TPU v7x, 32 devices: a whole 2x2x4 slice. The times are simulated.
32 devices in a mesh: cohort: 2 (over y), bx: 16 (over z, x, core).
Axes of the slice: x: 2, y: 2, z: 4, core: 2. Of those that a mesh axis runs over, the one named last changes fastest.
Arguments:
- bold: bfloat16 [256, 12, 4096], P('cohort', None, 'bx'), parts along dimension 0, may hold values from -6 to 6
- nbr_table: int32 [256, 4096], P('cohort', 'bx'), parts along dimension 0, may hold values from -1 to 767, as said below
- subject: int32 [256], P('cohort'), parts along dimension 0, may hold values from 0 to 7
Outputs:
- spread: float32 [8192], P(('cohort', 'bx')), parts along dimension 0
- gram_mean: float32 [256, 128], P('cohort'), parts along dimension 0
There are 2 independent parts, one for each index of `cohort`. A program takes and returns all parts, laid end to end along the dimension named above; each array names one. Nothing has to cross between parts.
Inputs may be any that keep to these rules, and one draw needn't show every extreme that they name: `nbr_table`: rows 125 to 127 are all -1 and row (124) // 2 names the centre itself (256 + its place in its block). Any other entry is -1 or the place, in the window made of the previous block, the centre's own block and the next block (768 voxels in order), of a voxel at most 147 voxels away from the centre in voxel order; no entry names a voxel outside the cohort's 4096 voxels.
All inputs are finite; a program needn't handle non-finite values.
Results may differ from a plain program's by a relative error of at most 0.0003.
Values may be sent and summed in bfloat16 or wider, within the bound.
A program may use at most 64 MiB of HBM per device.

v0:
```python
import jax
import jax.numpy as jnp
from jax import lax
from jax.sharding import PartitionSpec as P

NB = 125
SUBJ = 8


VARIANCE_FLOOR = 0.05


def extended(cells, sides, width):
    for axis, dim in sides:
        count = lax.axis_size(axis)
        ends = count - 1
        head = lax.slice_in_dim(cells, 0, width, axis=dim)
        tail = lax.slice_in_dim(cells, cells.shape[dim] - width, cells.shape[dim], axis=dim)
        cells = jnp.concatenate(
            [
                lax.ppermute(tail, axis, [(i, (i + 1) % count) for i in range(ends)]),
                cells,
                lax.ppermute(head, axis, [((i + 1) % count, i) for i in range(ends)]),
            ],
            axis=dim,
        )
    return cells


def normalize(series):
    values = series.astype(jnp.float32)
    centred = values - jnp.mean(values, axis=1, keepdims=True)
    divisor = jnp.sqrt(jnp.sum(centred * centred, axis=1, keepdims=True) + 1.0)
    return (centred / divisor).astype(jnp.bfloat16)


def zscore(correl, onehot, counts):
    averages = (
        jnp.einsum("es,ecj->scj", onehot, correl, precision=lax.Precision.HIGHEST)
        / counts[:, None, None]
    )
    expanded = jnp.einsum("es,scj->ecj", onehot, averages, precision=lax.Precision.HIGHEST)
    deviation = correl - expanded
    variance = (
        jnp.einsum("es,ecj->scj", onehot, deviation * deviation, precision=lax.Precision.HIGHEST)
        / counts[:, None, None]
    )
    divisor = jnp.einsum(
        "es,scj->ecj", onehot, jnp.sqrt(variance + VARIANCE_FLOOR), precision=lax.Precision.HIGHEST
    )
    return deviation / divisor


def per_device(bold, nbr_table, subject):
    epochs, points, block_len = bold.shape
    normed = normalize(bold)
    window = extended(normed, (("bx", 2),), block_len)
    window_len = window.shape[2]
    onehot = (subject[:, None] == jnp.arange(SUBJ, dtype=jnp.int32)[None, :]).astype(jnp.float32)
    counts = jnp.maximum(jnp.sum(onehot, axis=0), 1.0)
    group_len = 16
    group_count = block_len // group_len
    places = jnp.arange(window_len, dtype=jnp.int32)

    def one_group(running, group_id):
        first_col = group_id * group_len
        lookup = lax.dynamic_slice_in_dim(nbr_table, first_col, group_len, 1).T
        relative = jnp.where(lookup >= 0, lookup, -1)
        selector = (relative[:, :, None] == places[None, None, :]).astype(jnp.float32)
        centre = lax.dynamic_slice_in_dim(normed, first_col, group_len, 2)
        products = jnp.einsum("etc,etw->ecw", centre, window, preferred_element_type=jnp.float32)
        correl = jnp.einsum("ecw,cjw->ecj", products, selector, precision=lax.Precision.HIGHEST)
        features = zscore(correl, onehot, counts)
        kernel = (
            jnp.einsum("ecj,fcj->cef", features, features, precision=lax.Precision.HIGHEST) / NB
        )
        return (
            running + jnp.sum(kernel, axis=0),
            jnp.sqrt(jnp.sum(kernel * kernel, axis=(1, 2)) / epochs),
        )

    totals, spread = lax.scan(
        one_group,
        jnp.zeros((epochs, epochs), jnp.float32),
        jnp.arange(group_count, dtype=jnp.int32),
    )
    divisor = block_len * lax.axis_size("bx")
    gram_mean = lax.psum(totals, "bx") / divisor
    return (spread.reshape(-1), gram_mean)


def solution(mesh):
    return jax.shard_map(
        per_device,
        mesh=mesh,
        in_specs=(P("cohort", None, "bx"), P("cohort", "bx"), P("cohort")),
        out_specs=(P(("cohort", "bx")), P("cohort", None)),
        check_vma=False,
    )
```

profile of v0, /device:TPU:0, one launch (start us, length us, event | category | flops | bytes accessed | tf_op | source)
XLA Modules:
  0.0 409.4 jit_solution(16473115534681401956)
XLA Ops:
  11.3 2.4 collective-permute-start
  15.6 4.4 %collective-permute-done.1 = bf16[128,12,256]{2,0,1:T(8,128)(2,1)S(1)} collective-permute-done((bf16[128,12,256]{2,0,1:T(8,128)(2,1)S(1)}, bf16[128,12,256]{2,0,1:T(8,128)(2,1)S(1)}, u32[]{:S(2)}, u32[]{:S(2)}) %collective-permute-start.1) | collective-permute-done | bytes 786464 | tf_op jit(solution)/shard_map/ppermute | solution.py:23
  21.5 277.3 %while.13 = (s32[]{:T(128)}, f32[128,128]{1,0:T(8,128)S(1)}, f32[16,16]{1,0:T(8,128)S(1)}, s32[16]{0:T(128)S(1)}, s32[128,256]{0,1:T(8,128)S(1)}, /*index=5*/bf1...) while((s32[]{:T(128)}, f32[128,128]{1,0:T(8,128)S(1)}, ...), condition=%wide.region_6.7_spmd.clone, body=%wide.region_3.6_spmd.clone.sunk | while | flops 2960470016 | bytes 24029772 | solution.py:82
  25.3 6.0 %fusion.74 = f32[128,16,128]{0,2,1:T(8,128)S(1)} fusion(f32[128,16,768]{2,1,0:T(8,128)S(1)} %fusion.73, s32[16,128]{1,0:T(8,128)S(1)} %compare_select_fusion.2), kind=kOutput, calls=%fused_computation.6.clone.1 | convolution fusion | flops 2417491968 | bytes 7348224 | tf_op jit(solution)/shard_map/while/body/eval_jaxpr/ecw,cjw->ecj/dot_general | solution.py:72
  37.0 1.9 multiply_reduce_fusion.2
  42.6 6.0 %fusion.74 = f32[128,16,128]{0,2,1:T(8,128)S(1)} fusion(f32[128,16,768]{2,1,0:T(8,128)S(1)} %fusion.73, s32[16,128]{1,0:T(8,128)S(1)} %compare_select_fusion.2), kind=kOutput, calls=%fused_computation.6.clone.1 | convolution fusion | flops 2417491968 | bytes 7348224 | tf_op jit(solution)/shard_map/while/body/eval_jaxpr/ecw,cjw->ecj/dot_general | solution.py:72
  54.3 1.9 multiply_reduce_fusion.2
  59.9 6.0 %fusion.74 = f32[128,16,128]{0,2,1:T(8,128)S(1)} fusion(f32[128,16,768]{2,1,0:T(8,128)S(1)} %fusion.73, s32[16,128]{1,0:T(8,128)S(1)} %compare_select_fusion.2), kind=kOutput, calls=%fused_computation.6.clone.1 | convolution fusion | flops 2417491968 | bytes 7348224 | tf_op jit(solution)/shard_map/while/body/eval_jaxpr/ecw,cjw->ecj/dot_general | solution.py:72
  71.6 1.9 multiply_reduce_fusion.2
  77.2 6.0 %fusion.74 = f32[128,16,128]{0,2,1:T(8,128)S(1)} fusion(f32[128,16,768]{2,1,0:T(8,128)S(1)} %fusion.73, s32[16,128]{1,0:T(8,128)S(1)} %compare_select_fusion.2), kind=kOutput, calls=%fused_computation.6.clone.1 | convolution fusion | flops 2417491968 | bytes 7348224 | tf_op jit(solution)/shard_map/while/body/eval_jaxpr/ecw,cjw->ecj/dot_general | solution.py:72
  94.5 6.0 %fusion.74 = f32[128,16,128]{0,2,1:T(8,128)S(1)} fusion(f32[128,16,768]{2,1,0:T(8,128)S(1)} %fusion.73, s32[16,128]{1,0:T(8,128)S(1)} %compare_select_fusion.2), kind=kOutput, calls=%fused_computation.6.clone.1 | convolution fusion | flops 2417491968 | bytes 7348224 | tf_op jit(solution)/shard_map/while/body/eval_jaxpr/ecw,cjw->ecj/dot_general | solution.py:72
  111.9 6.0 %fusion.74 = f32[128,16,128]{0,2,1:T(8,128)S(1)} fusion(f32[128,16,768]{2,1,0:T(8,128)S(1)} %fusion.73, s32[16,128]{1,0:T(8,128)S(1)} %compare_select_fusion.2), kind=kOutput, calls=%fused_computation.6.clone.1 | convolution fusion | flops 2417491968 | bytes 7348224 | tf_op jit(solution)/shard_map/while/body/eval_jaxpr/ecw,cjw->ecj/dot_general | solution.py:72
  129.2 6.0 %fusion.74 = f32[128,16,128]{0,2,1:T(8,128)S(1)} fusion(f32[128,16,768]{2,1,0:T(8,128)S(1)} %fusion.73, s32[16,128]{1,0:T(8,128)S(1)} %compare_select_fusion.2), kind=kOutput, calls=%fused_computation.6.clone.1 | convolution fusion | flops 2417491968 | bytes 7348224 | tf_op jit(solution)/shard_map/while/body/eval_jaxpr/ecw,cjw->ecj/dot_general | solution.py:72
  146.5 6.0 %fusion.74 = f32[128,16,128]{0,2,1:T(8,128)S(1)} fusion(f32[128,16,768]{2,1,0:T(8,128)S(1)} %fusion.73, s32[16,128]{1,0:T(8,128)S(1)} %compare_select_fusion.2), kind=kOutput, calls=%fused_computation.6.clone.1 | convolution fusion | flops 2417491968 | bytes 7348224 | tf_op jit(solution)/shard_map/while/body/eval_jaxpr/ecw,cjw->ecj/dot_general | solution.py:72
  163.8 6.0 %fusion.74 = f32[128,16,128]{0,2,1:T(8,128)S(1)} fusion(f32[128,16,768]{2,1,0:T(8,128)S(1)} %fusion.73, s32[16,128]{1,0:T(8,128)S(1)} %compare_select_fusion.2), kind=kOutput, calls=%fused_computation.6.clone.1 | convolution fusion | flops 2417491968 | bytes 7348224 | tf_op jit(solution)/shard_map/while/body/eval_jaxpr/ecw,cjw->ecj/dot_general | solution.py:72
  181.2 6.0 %fusion.74 = f32[128,16,128]{0,2,1:T(8,128)S(1)} fusion(f32[128,16,768]{2,1,0:T(8,128)S(1)} %fusion.73, s32[16,128]{1,0:T(8,128)S(1)} %compare_select_fusion.2), kind=kOutput, calls=%fused_computation.6.clone.1 | convolution fusion | flops 2417491968 | bytes 7348224 | tf_op jit(solution)/shard_map/while/body/eval_jaxpr/ecw,cjw->ecj/dot_general | solution.py:72
  198.5 6.0 %fusion.74 = f32[128,16,128]{0,2,1:T(8,128)S(1)} fusion(f32[128,16,768]{2,1,0:T(8,128)S(1)} %fusion.73, s32[16,128]{1,0:T(8,128)S(1)} %compare_select_fusion.2), kind=kOutput, calls=%fused_computation.6.clone.1 | convolution fusion | flops 2417491968 | bytes 7348224 | tf_op jit(solution)/shard_map/while/body/eval_jaxpr/ecw,cjw->ecj/dot_general | solution.py:72
  215.8 6.0 %fusion.74 = f32[128,16,128]{0,2,1:T(8,128)S(1)} fusion(f32[128,16,768]{2,1,0:T(8,128)S(1)} %fusion.73, s32[16,128]{1,0:T(8,128)S(1)} %compare_select_fusion.2), kind=kOutput, calls=%fused_computation.6.clone.1 | convolution fusion | flops 2417491968 | bytes 7348224 | tf_op jit(solution)/shard_map/while/body/eval_jaxpr/ecw,cjw->ecj/dot_general | solution.py:72
  233.1 6.0 %fusion.74 = f32[128,16,128]{0,2,1:T(8,128)S(1)} fusion(f32[128,16,768]{2,1,0:T(8,128)S(1)} %fusion.73, s32[16,128]{1,0:T(8,128)S(1)} %compare_select_fusion.2), kind=kOutput, calls=%fused_computation.6.clone.1 | convolution fusion | flops 2417491968 | bytes 7348224 | tf_op jit(solution)/shard_map/while/body/eval_jaxpr/ecw,cjw->ecj/dot_general | solution.py:72
  250.4 6.0 %fusion.74 = f32[128,16,128]{0,2,1:T(8,128)S(1)} fusion(f32[128,16,768]{2,1,0:T(8,128)S(1)} %fusion.73, s32[16,128]{1,0:T(8,128)S(1)} %compare_select_fusion.2), kind=kOutput, calls=%fused_computation.6.clone.1 | convolution fusion | flops 2417491968 | bytes 7348224 | tf_op jit(solution)/shard_map/while/body/eval_jaxpr/ecw,cjw->ecj/dot_general | solution.py:72
  267.8 6.0 %fusion.74 = f32[128,16,128]{0,2,1:T(8,128)S(1)} fusion(f32[128,16,768]{2,1,0:T(8,128)S(1)} %fusion.73, s32[16,128]{1,0:T(8,128)S(1)} %compare_select_fusion.2), kind=kOutput, calls=%fused_computation.6.clone.1 | convolution fusion | flops 2417491968 | bytes 7348224 | tf_op jit(solution)/shard_map/while/body/eval_jaxpr/ecw,cjw->ecj/dot_general | solution.py:72
  285.1 6.0 %fusion.74 = f32[128,16,128]{0,2,1:T(8,128)S(1)} fusion(f32[128,16,768]{2,1,0:T(8,128)S(1)} %fusion.73, s32[16,128]{1,0:T(8,128)S(1)} %compare_select_fusion.2), kind=kOutput, calls=%fused_computation.6.clone.1 | convolution fusion | flops 2417491968 | bytes 7348224 | tf_op jit(solution)/shard_map/while/body/eval_jaxpr/ecw,cjw->ecj/dot_general | solution.py:72
  296.8 1.9 multiply_reduce_fusion.2
  300.1 100.9 %all-reduce.2.cloned.1.call-done = f32[128,128]{1,0:T(8,128)} async-done(((f32[128,128]{1,0:T(8,128)}), f32[128,128]{1,0:T(8,128)}) %all-reduce.2.cloned.1.call-update) | async-done | bytes 65552 | tf_op jit(solution)/shard_map/psum | solution.py:88
  (215 shorter events, 171.3 us)
Async XLA Ops:
  7.2 7.9 %copy-start.2 = (s32[128,256]{1,0:T(8,128)S(1)}, s32[128,256]{1,0:T(8,128)}, u32[]{:S(2)}) copy-start(s32[128,256]{1,0:T(8,128)} %param.6) | copy-start | bytes 393220
  7.2 8.0 %copy-start.3 = (s32[128]{0:T(128)S(1)}, s32[128]{0:T(128)}, u32[]{:S(2)}) copy-start(s32[128]{0:T(128)} %param.7) | copy-start | bytes 1540
  7.2 393.9 %all-reduce.2.cloned.1.call-start = ((), (), s32[]{:S(2)}) async-start(), calls=%async_computation | async-start | bytes 131072 | tf_op jit(solution)/shard_map/psum | solution.py:88
  11.3 8.7 %copy-start = (bf16[128,12,256]{2,0,1:T(8,128)(2,1)}, bf16[128,12,256]{2,0,1:T(8,128)(2,1)S(1)}, u32[]{:S(2)}) copy-start(bf16[128,12,256]{2,0,1:T(8,128)(2,1)S(1)} %fusion.34) | copy-start | bytes 2359300
  11.3 4.3 %collective-permute-start = (bf16[128,12,256]{2,0,1:T(8,128)(2,1)S(1)}, bf16[128,12,256]{2,0,1:T(8,128)(2,1)S(1)}, u32[]{:S(2)}, u32[]{:S(2)}) collective-permute-start(bf16[128,12,256]{2,0,1:T(8,128)(2,1)S(1)} %fusion.34), channel_id=1, source_target_pairs={{0,1},{1,2},{2,3},{3,4},{4,5},{5,6},{6,7},{7,8},{8,9},{9,10},{10,1... | collective-permute-start | bytes 2359304 | tf_op jit(solution)/shard_map/ppermute | solution.py:21
  13.7 6.2 %collective-permute-start.1 = (bf16[128,12,256]{2,0,1:T(8,128)(2,1)S(1)}, bf16[128,12,256]{2,0,1:T(8,128)(2,1)S(1)}, u32[]{:S(2)}, u32[]{:S(2)}) collective-permute-start(bf16[128,12,256]{2,0,1:T(8,128)(2,1)S(1)} %fusion.34), channel_id=1, source_target_pairs={{1,0},{2,1},{3,2},{4,3},{5,4},{6,5},{7,6},{8,7},{9,8},{10,9},{11,1... | collective-permute-start | bytes 2359304 | tf_op jit(solution)/shard_map/ppermute | solution.py:23
  298.8 0.6 copy-start.1
Sparse Core Ops, SparseCore 0:
  299.6 101.3 all-reduce.1
where the time goes:
time: 411 us; the launch traced here: 409 us
  matrix products  236 us (57%)
  waiting for transfers between devices  106 us (26%)
  local copies, waits for them, and re-layouts  31.5 us (8%)
  between operations  14.2 us (3%)
  loops' own time  11.9 us (3%)
  other arithmetic  6.57 us (2%)
    psum x1, waiting for transfers between devices, per_device(): gram_mean = lax.psum(totals, 'bx') / divisor  101 us
    dot_general x16, matrix products, one_group(): jnp.einsum('ecw,cjw->ecj', products, selector, precision=lax.Precision.HI...  96.5 us
    dot_general x16, matrix products, one_group(): jnp.einsum('ecj,fcj->cef', features, features, precision=lax.Precision.HI...  31 us
    dot_general x16, matrix products, zscore(): jnp.einsum('es,scj->ecj', onehot, averages, precision=lax.Precision.HIGHEST)  29.2 us
    dot_general x16, matrix products, zscore(): jnp.einsum('es,scj->ecj', onehot, jnp.sqrt(variance + VARIANCE_FLOOR), pr...  29 us
    dynamic_slice x16, local copies, waits for them, and re-layouts, one_group(): centre = lax.dynamic_slice_in_dim(normed, first_col, group_len, 2)  18.8 us
    dot_general x16, matrix products, one_group(): jnp.einsum('etc,etw->ecw', centre, window, preferred_element_type=jnp.flo...  18 us
    dot_general x16, matrix products, zscore(): jnp.einsum('es,ecj->scj', onehot, deviation * deviation, precision=lax.Pr...  16.4 us
  transfers between devices with their start and end apart: 3, of which 3 were waited for; matrix products, arithmetic and copies ran while one was open for 0% of the time, Pallas kernels for 0%

commit v1 on v0

v1 whole, which is shorter than its diff:
```python
import functools

import jax
import jax.numpy as jnp
from jax import lax
from jax.experimental import pallas as pl
from jax.experimental.pallas import tpu as pltpu
from jax.sharding import PartitionSpec as P

NB = 125
SUBJ = 8
REACH = 147
VARIANCE_FLOOR = 0.05

SLOTS = 16
GROUP = 16
CHUNK = 64
LANES = 128
LEAD = 160
SPAN = 384


def normalize(series):
    values = series.astype(jnp.float32)
    centred = values - jnp.mean(values, axis=1, keepdims=True)
    divisor = jnp.sqrt(jnp.sum(centred * centred, axis=1, keepdims=True) + 1.0)
    return (centred / divisor).astype(jnp.bfloat16)


def features_kernel(win_ref, own_ref, idx_ref, sid_ref, hot_ref, inv_ref, keep_ref,
                    square_ref, gram_ref, lhs_ref, prod_ref, mean_ref):
    chunk = pl.program_id(0)
    first = chunk * CHUNK
    parity = lax.rem(chunk, 2)
    start = pl.multiple_of((chunk // 2) * LANES, LANES)
    epochs = gram_ref.shape[0]
    depth = GROUP * SLOTS
    groups = epochs // GROUP

    row_epoch = lax.broadcasted_iota(jnp.int32, (GROUP, depth), 0)
    col_epoch = lax.broadcasted_iota(jnp.int32, (GROUP, depth), 1) // SLOTS
    diagonal = row_epoch == col_epoch

    @pl.when(chunk == 0)
    def _():
        gram_ref[...] = jnp.zeros_like(gram_ref)

    def one_group(g, carry):
        cols = pl.ds(pl.multiple_of(g * depth, depth), depth)
        for c in range(CHUNK):
            row = jnp.broadcast_to(own_ref[pl.ds(first + c, 1), cols], (GROUP, depth))
            lhs_ref[c * GROUP:(c + 1) * GROUP, :] = jnp.where(diagonal, row, 0.0).astype(jnp.bfloat16)
        prod = jnp.dot(lhs_ref[...], win_ref[parity, cols, pl.ds(start, SPAN)],
                       preferred_element_type=jnp.float32)
        prod_ref[:, pl.ds(pl.multiple_of(g * GROUP, GROUP), GROUP), :] = prod.reshape(CHUNK, GROUP, SPAN)
        for c in range(CHUNK // 2):
            pair = []
            for i in range(2):
                row = jnp.broadcast_to(own_ref[pl.ds(first + 2 * c + i, 1), cols], (SUBJ, depth))
                pair.append(row * keep_ref[:, cols])
            lhs_ref[c * GROUP:(c + 1) * GROUP, :] = jnp.concatenate(pair, axis=0).astype(jnp.bfloat16)
        part = jnp.dot(lhs_ref[:CHUNK * SUBJ, :], win_ref[parity, cols, pl.ds(start, SPAN)],
                       preferred_element_type=jnp.float32).reshape(CHUNK, SUBJ, SPAN)

        @pl.when(g == 0)
        def _():
            mean_ref[...] = part

        @pl.when(g > 0)
        def _():
            mean_ref[...] += part
        return carry

    lax.fori_loop(0, groups, one_group, 0)

    inv = inv_ref[...]

    def select(ref, c, lane, tile, rows):
        out = jnp.zeros((rows, LANES), jnp.float32)
        at = jnp.broadcast_to(lane, (rows, LANES))
        for t in range(SPAN // LANES):
            got = jnp.take_along_axis(ref[c, :, t * LANES:(t + 1) * LANES], at, axis=1,
                                      mode="promise_in_bounds")
            out = jnp.where(jnp.broadcast_to(tile == t, (rows, LANES)), got, out)
        return out

    def expand(stat):
        return jnp.concatenate(
            [jnp.take_along_axis(stat, sid_ref[r * 8:(r + 1) * 8, :], axis=0, mode="promise_in_bounds")
             for r in range(epochs // 8)], axis=0)

    def one_pair(p, carry):
        devs, sqs = [], []
        for i in range(2):
            c = 2 * p + i
            raw = idx_ref[pl.ds(first + c, 1), :]
            local = raw - (2 * LANES + first - LEAD)
            lane = local & (LANES - 1)
            tile = jnp.where(raw < 0, -1, local >> 7)
            correl = select(prod_ref, c, lane, tile, epochs)
            mean = select(mean_ref, c, lane, tile, SUBJ) * inv
            dev = correl - expand(mean)
            devs.append(dev)
            sqs.append((dev * dev).astype(jnp.bfloat16))
        var = jnp.dot(hot_ref[...], jnp.concatenate(sqs, axis=1), preferred_element_type=jnp.float32)[:SUBJ]
        total = None
        for i in range(2):
            scale = lax.rsqrt(var[:, i * LANES:(i + 1) * LANES] * inv + VARIANCE_FLOOR)
            feat = (devs[i] * expand(scale)).astype(jnp.bfloat16)
            kern = lax.dot_general(feat, feat, (((1,), (1,)), ((), ())), preferred_element_type=jnp.float32)
            square_ref[pl.ds(first + 2 * p + i, 1), :] = jnp.sum(kern * kern, axis=0, keepdims=True)
            total = kern if total is None else total + kern
        gram_ref[...] += total
        return carry

    lax.fori_loop(0, CHUNK // 2, one_pair, 0)


def per_device(bold, nbr_table, subject):
    epochs, points, block_len = bold.shape
    count = lax.axis_size("bx")
    normed = jnp.pad(normalize(bold), ((0, 0), (0, SLOTS - points), (0, 0)))
    left = lax.ppermute(normed[:, :, block_len - LEAD:], "bx", [(i, i + 1) for i in range(count - 1)])
    right = lax.ppermute(normed[:, :, :LEAD], "bx", [(i + 1, i) for i in range(count - 1)])
    ext = jnp.concatenate([left, normed, right], axis=2).reshape(epochs * SLOTS, -1)
    wide = SPAN + LANES
    win = jnp.stack([ext[:, :wide], ext[:, CHUNK:CHUNK + wide]])
    own = normed.reshape(epochs * SLOTS, block_len).T.astype(jnp.float32)
    onehot = subject[None, :] == jnp.arange(SUBJ, dtype=jnp.int32)[:, None]
    counts = jnp.maximum(jnp.sum(onehot.astype(jnp.float32), axis=1), 1.0)
    inv = jnp.broadcast_to((1.0 / counts)[:, None], (SUBJ, LANES))
    sid = jnp.broadcast_to(subject[:, None], (epochs, LANES))
    hot = jnp.pad(onehot.astype(jnp.bfloat16), ((0, 8), (0, 0)))
    keep = jnp.repeat(onehot.astype(jnp.float32), SLOTS, axis=1)
    vmem = pl.BlockSpec(memory_space=pltpu.VMEM)
    squares, total = pl.pallas_call(
        features_kernel,
        grid=(block_len // CHUNK,),
        in_specs=[vmem] * 7,
        out_specs=[vmem] * 2,
        out_shape=[jax.ShapeDtypeStruct((block_len, epochs), jnp.float32),
                   jax.ShapeDtypeStruct((epochs, epochs), jnp.float32)],
        scratch_shapes=[
            pltpu.VMEM((CHUNK * GROUP, GROUP * SLOTS), jnp.bfloat16),
            pltpu.VMEM((CHUNK, epochs, SPAN), jnp.float32),
            pltpu.VMEM((CHUNK, SUBJ, SPAN), jnp.float32),
        ],
        compiler_params=pltpu.CompilerParams(dimension_semantics=("arbitrary",),
                                             vmem_limit_bytes=60 * 1024 * 1024),
        name="features",
    )(win, own, nbr_table.T, sid, hot, inv, keep)
    spread = jnp.sqrt(jnp.sum(squares, axis=1) / (epochs * NB * NB))
    gram_mean = lax.psum(total, "bx") / (NB * block_len * count)
    return spread, gram_mean


def solution(mesh):
    return jax.shard_map(
        per_device,
        mesh=mesh,
        in_specs=(P("cohort", None, "bx"), P("cohort", "bx"), P("cohort")),
        out_specs=(P(("cohort", "bx")), P("cohort", None)),
        check_vma=False,
    )
```

time: 411 us -> 245 us (0.60)
  matrix products: 236 us -> 0 us
  Pallas kernels: 0 us -> 104 us
  local copies, waits for them, and re-layouts: 31.5 us -> 13.8 us
  loops' own time: 11.9 us -> 0 us
  waiting for transfers between devices: 106 us -> 94.8 us
  other arithmetic: 6.57 us -> 12.2 us
    dot_general x112 -> x0, matrix products: 236 us -> none  [the longest x16 96.5 us: one_group(): jnp.einsum('ecw,cjw->ecj', products, selector, precision=lax.Precision.HI...]
    pallas_call x0 -> x1, Pallas kernels: none -> 104 us  [per_device(): pl.pallas_call(features_kernel, grid=(block_len // CHUNK,), in_specs=[vme...]
    dynamic_slice x32 -> x0, local copies, waits for them, and re-layouts: 28.1 us -> none  [the longest x16 18.8 us: one_group(): centre = lax.dynamic_slice_in_dim(normed, first_col, group_len, 2)]
    another operation x1 -> x0, loops' own time: 11.9 us -> none  [per_device(): lax.scan(one_group, jnp.zeros((epochs, epochs), jnp.float32), jnp.arange(...]
    psum x1, waiting for transfers between devices: 101 us -> 94.8 us  [per_device(): gram_mean = lax.psum(total, 'bx') / (NB * block_len * count)]
    ppermute x2, waiting for transfers between devices: 4.67 us -> 0.01 us  [the longest x1 0.01 us: per_device(): lax.ppermute(normed[:, :, block_len - LEAD:], 'bx', [(i, i + 1) for i in...]
  transfers between devices with their start and end apart: 3 -> 3, of which waited for: 3 -> 1; matrix products, arithmetic and copies ran while one was open for 0% -> 4% of each run, Pallas kernels for 0% -> 0%
where the time goes in v1:
time: 245 us; the launch traced here: 244 us
  Pallas kernels  104 us (42%)
  waiting for transfers between devices  94.8 us (39%)
  between operations  14.2 us (6%)
  local copies, waits for them, and re-layouts  13.8 us (6%)
  other arithmetic  12.2 us (5%)
  starting transfers between devices  4.56 us (2%)
    pallas_call x1, Pallas kernels, per_device(): pl.pallas_call(features_kernel, grid=(block_len // CHUNK,), in_specs=[vme...  104 us
    psum x1, waiting for transfers between devices, per_device(): gram_mean = lax.psum(total, 'bx') / (NB * block_len * count)  94.8 us
  transfers between devices with their start and end apart: 3, of which 1 were waited for; matrix products, arithmetic and copies ran while one was open for 4% of the time, Pallas kernels for 0%

profile of v1, /device:TPU:0, one launch (start us, length us, event | category | flops | bytes accessed | tf_op | source)
XLA Modules:
  0.0 243.8 jit_solution(10473872676436512918)
XLA Ops:
  7.2 2.0 convert_reduce_fusion
  9.2 2.0 fusion.2
  11.3 0.7 fusion.3
  11.9 0.6 pad_slice_fusion.1
  12.5 1.6 copy.12
  14.1 3.2 %collective-permute-start = (bf16[128,16,160]{0,2,1:T(8,128)(2,1)}, bf16[128,16,160]{0,2,1:T(8,128)(2,1)}, u32[]{:S(2)}, u32[]{:S(2)}) collective-permute-start(bf16[128,16,160]{0,2,1:T(8,128)(2,1)} %copy.12), channel_id=1, source_target_pairs={{0,1},{1,2},{2,3},{3,4},{4,5},{5,6},{6,7},{7,8},{8,9},{9,10},{10,1... | collective-permute-start | bytes 1966088 | tf_op jit(solution)/shard_map/ppermute | solution.py:123
  17.4 1.6 copy.13
  19.0 1.3 collective-permute-start.1
  20.6 1.9 copy.16
  22.7 0.9 reshape.30.keep_ref
  23.6 0.7 copy.17
  24.5 0.6 pad_convert_fusion.hot_ref
  25.1 1.8 copy.14
  26.9 1.8 copy.15
  28.7 1.3 pad_maximum_fusion.1
  29.9 1.2 slice_bitcast_fusion.1
  31.2 2.3 pad_maximum_fusion.win_ref
  33.4 0.7 broadcast_in_dim.6.sid_ref
  34.2 0.7 broadcast_in_dim.7.inv_ref
  34.8 104.3 %features.1 = (f32[256,128]{1,0:T(8,128)}, f32[128,128]{1,0:T(8,128)}) custom-call(bf16[2,2048,512]{2,1,0:T(8,128)(2,1)} %pad_maximum_fusion.win_ref, f32[256,2048]{1,0:T(8,128)} %bitcast.11, s32[256,128]{1,0:T(8,128)} %bitcast.12, s32[128,128]{1,0:T(8,128)} %broadcast_in_dim.6.sid_ref, bf16[16,128]{1,0:T(8,128)(2,1)} %pad_convert_fusion.hot_ref, ...), custom_call_target="tpu_custom_call" | custom-call | tf_op jit(solution)/shard_map/features/pallas_call | solution.py:136
  139.2 1.0 reduce_sum.39
  140.2 0.6 multiply_sqrt_fusion
  140.7 94.8 %all-reduce.4.cloned.1.call-done = f32[128,128]{1,0:T(8,128)} async-done(((f32[128,128]{1,0:T(8,128)}), f32[128,128]{1,0:T(8,128)}) %all-reduce.4.cloned.1.call-update) | async-done | bytes 65552 | tf_op jit(solution)/shard_map/psum | solution.py:153
  235.5 1.5 broadcast_multiply_fusion.1
  (18 shorter events, 0.8 us)
Async XLA Ops:
  7.2 4.1 %copy-start = (bf16[128,12,256]{2,0,1:T(8,128)(2,1)S(1)}, bf16[128,12,256]{2,0,1:T(8,128)(2,1)}, u32[]{:S(2)}) copy-start(bf16[128,12,256]{2,0,1:T(8,128)(2,1)} %param.3) | copy-start | bytes 2359300
  7.2 228.3 %all-reduce.4.cloned.1.call-start = ((), (), s32[]{:S(2)}) async-start(), calls=%async_computation | async-start | bytes 131072 | tf_op jit(solution)/shard_map/psum | solution.py:153
  14.1 10.9 %collective-permute-start = (bf16[128,16,160]{0,2,1:T(8,128)(2,1)}, bf16[128,16,160]{0,2,1:T(8,128)(2,1)}, u32[]{:S(2)}, u32[]{:S(2)}) collective-permute-start(bf16[128,16,160]{0,2,1:T(8,128)(2,1)} %copy.12), channel_id=1, source_target_pairs={{0,1},{1,2},{2,3},{3,4},{4,5},{5,6},{6,7},{7,8},{8,9},{9,10},{10,1... | collective-permute-start | bytes 1966088 | tf_op jit(solution)/shard_map/ppermute | solution.py:123
  19.0 7.9 %collective-permute-start.1 = (bf16[128,16,160]{0,2,1:T(8,128)(2,1)}, bf16[128,16,160]{0,2,1:T(8,128)(2,1)}, u32[]{:S(2)}, u32[]{:S(2)}) collective-permute-start(bf16[128,16,160]{0,2,1:T(8,128)(2,1)} %copy.13), channel_id=1, source_target_pairs={{1,0},{2,1},{3,2},{4,3},{5,4},{6,5},{7,6},{8,7},{9,8},{10,9},{11,1... | collective-permute-start | bytes 1966088 | tf_op jit(solution)/shard_map/ppermute | solution.py:124
  20.6 1.9 copy-start.2
  20.6 3.0 %copy-start.1 = (s32[128,256]{1,0:T(8,128)S(1)}, s32[128,256]{1,0:T(8,128)}, u32[]{:S(2)}) copy-start(s32[128,256]{1,0:T(8,128)} %param.4) | copy-start | bytes 393220
Sparse Core Ops, SparseCore 0:
  139.3 96.1 all-reduce.3

commit v2 on v1

--- a/solution.py
+++ b/solution.py
@@ -18,6 +18,8 @@
 LANES = 128
 LEAD = 160
 SPAN = 384
+BATCH = 4
+MESH = pl.DeviceIdType.MESH
 
 
 def normalize(series):
@@ -28,7 +30,7 @@
 
 
 def features_kernel(win_ref, own_ref, idx_ref, sid_ref, hot_ref, inv_ref, keep_ref,
-                    square_ref, gram_ref, lhs_ref, prod_ref, mean_ref):
+                    square_ref, gram_ref, lhs_ref, prod_ref, mean_ref, root_ref, sq_ref, feat_ref, var_ref):
     chunk = pl.program_id(0)
     first = chunk * CHUNK
     parity = lax.rem(chunk, 2)
@@ -44,6 +46,25 @@
     @pl.when(chunk == 0)
     def _():
         gram_ref[...] = jnp.zeros_like(gram_ref)
+        slots, block_len = idx_ref.shape
+        for half in range(block_len // LANES):
+            place = lax.broadcasted_iota(jnp.int32, (1, LANES), 1) + half * LANES
+            shift = block_len - LEAD + place // CHUNK * CHUNK
+
+            def one_tile(w, carry):
+                at = lax.broadcasted_iota(jnp.int32, (32, LANES), 0) + w * 32
+                hits = jnp.zeros((32, LANES), jnp.float32)
+                for j in range(NB):
+                    rel = idx_ref[j:j + 1, half * LANES:(half + 1) * LANES] - shift
+                    hits = hits + jnp.where(jnp.broadcast_to(rel, (32, LANES)) == at, 1.0, 0.0)
+                lhs = jnp.sqrt(hits)
+                mean_ref[pl.ds(w * 4, 4), :, :LANES] = lhs.reshape(4, 8, LANES)
+                return carry
+
+            lax.fori_loop(0, SPAN // 32, one_tile, 0)
+            for t in range(SPAN // LANES):
+                tile = mean_ref[t * 16:(t + 1) * 16, :, :LANES].reshape(LANES, LANES)
+                root_ref[half * LANES:(half + 1) * LANES, t * LANES:(t + 1) * LANES] = tile.T
 
     def one_group(g, carry):
         cols = pl.ds(pl.multiple_of(g * depth, depth), depth)
@@ -73,47 +94,110 @@
 
     lax.fori_loop(0, groups, one_group, 0)
 
-    inv = inv_ref[...]
-
-    def select(ref, c, lane, tile, rows):
-        out = jnp.zeros((rows, LANES), jnp.float32)
-        at = jnp.broadcast_to(lane, (rows, LANES))
-        for t in range(SPAN // LANES):
-            got = jnp.take_along_axis(ref[c, :, t * LANES:(t + 1) * LANES], at, axis=1,
-                                      mode="promise_in_bounds")
-            out = jnp.where(jnp.broadcast_to(tile == t, (rows, LANES)), got, out)
-        return out
-
-    def expand(stat):
+    inv = jnp.concatenate([inv_ref[...]] * (SPAN // LANES), axis=1)
+    feat_ref[...] = jnp.zeros_like(feat_ref)
+    steps = CHUNK // BATCH
+
+    def expand(stat, r):
+        at = sid_ref[r * 8:(r + 1) * 8, :]
         return jnp.concatenate(
-            [jnp.take_along_axis(stat, sid_ref[r * 8:(r + 1) * 8, :], axis=0, mode="promise_in_bounds")
-             for r in range(epochs // 8)], axis=0)
-
-    def one_pair(p, carry):
-        devs, sqs = [], []
-        for i in range(2):
-            c = 2 * p + i
-            raw = idx_ref[pl.ds(first + c, 1), :]
-            local = raw - (2 * LANES + first - LEAD)
-            lane = local & (LANES - 1)
-            tile = jnp.where(raw < 0, -1, local >> 7)
-            correl = select(prod_ref, c, lane, tile, epochs)
-            mean = select(mean_ref, c, lane, tile, SUBJ) * inv
-            dev = correl - expand(mean)
-            devs.append(dev)
-            sqs.append((dev * dev).astype(jnp.bfloat16))
-        var = jnp.dot(hot_ref[...], jnp.concatenate(sqs, axis=1), preferred_element_type=jnp.float32)[:SUBJ]
+            [jnp.take_along_axis(stat[:, t * LANES:(t + 1) * LANES], at, axis=0, mode="promise_in_bounds")
+             for t in range(SPAN // LANES)], axis=1)
+
+    def one_batch(p, carry):
+        base_c = jnp.maximum(p - 2, 0) * BATCH
+        base_b = jnp.clip(p - 1, 0, steps - 1) * BATCH
+        base_a = jnp.minimum(p, steps - 1) * BATCH
         total = None
-        for i in range(2):
-            scale = lax.rsqrt(var[:, i * LANES:(i + 1) * LANES] * inv + VARIANCE_FLOOR)
-            feat = (devs[i] * expand(scale)).astype(jnp.bfloat16)
+        for i in range(BATCH):
+            feat = feat_ref[i]
             kern = lax.dot_general(feat, feat, (((1,), (1,)), ((), ())), preferred_element_type=jnp.float32)
-            square_ref[pl.ds(first + 2 * p + i, 1), :] = jnp.sum(kern * kern, axis=0, keepdims=True)
+            square_ref[pl.ds(first + base_c + i, 1), :] = jnp.sum(kern * kern, axis=0, keepdims=True)
             total = kern if total is None else total + kern
         gram_ref[...] += total
+        for i in range(BATCH):
+            scale = lax.rsqrt(var_ref[i] * inv + VARIANCE_FLOOR) * root_ref[pl.ds(first + base_b + i, 1), :]
+            scale = jnp.where(p > 0, scale, 0.0)
+            for r in range(0, epochs // 8, 2):
+                pair = [prod_ref[base_b + i, (r + k) * 8:(r + k + 1) * 8, :] * expand(scale, r + k) for k in range(2)]
+                feat_ref[i, r * 8:(r + 2) * 8, :] = jnp.concatenate(pair, axis=0).astype(jnp.bfloat16)
+        for i in range(BATCH):
+            mean = mean_ref[base_a + i] * inv
+            for r in range(0, epochs // 8, 2):
+                pair = []
+                for k in range(2):
+                    rows = slice((r + k) * 8, (r + k + 1) * 8)
+                    dev = prod_ref[base_a + i, rows, :] - expand(mean, r + k)
+                    prod_ref[base_a + i, rows, :] = dev
+                    pair.append(dev * dev)
+                sq_ref[i, r * 8:(r + 2) * 8, :] = jnp.concatenate(pair, axis=0).astype(jnp.bfloat16)
+            var_ref[i] = jnp.dot(hot_ref[...], sq_ref[i], preferred_element_type=jnp.float32)[:SUBJ]
         return carry
 
-    lax.fori_loop(0, CHUNK // 2, one_pair, 0)
+    lax.fori_loop(0, steps + 2, one_batch, 0)
+
+
+def sum_kernel(count, part_ref, out_ref, took, send1, recv1, send2, recv2):
+    me = lax.axis_index("bx")
+    barrier = pltpu.get_barrier_semaphore()
+
+    def greet(d, carry):
+        pl.semaphore_signal(barrier, inc=1, device_id={"bx": lax.rem(me + d, count)}, device_id_type=MESH)
+        return carry
+
+    lax.fori_loop(1, count, greet, 0)
+    pl.semaphore_wait(barrier, count - 1)
+
+    def scatter(d):
+        to = lax.rem(me + d, count)
+        return pltpu.make_async_remote_copy(
+            src_ref=part_ref.at[to], dst_ref=took.at[d], send_sem=send1.at[d], recv_sem=recv1.at[d],
+            device_id={"bx": to}, device_id_type=MESH)
+
+    def gather(d):
+        return pltpu.make_async_remote_copy(
+            src_ref=out_ref.at[me], dst_ref=out_ref.at[me], send_sem=send2.at[d], recv_sem=recv2.at[d],
+            device_id={"bx": lax.rem(me + d, count)}, device_id_type=MESH)
+
+    def landed(d):
+        src = lax.rem(me + count - d, count)
+        return pltpu.make_async_remote_copy(
+            src_ref=out_ref.at[src], dst_ref=out_ref.at[src], send_sem=send2.at[d], recv_sem=recv2.at[d],
+            device_id={"bx": lax.rem(me + d, count)}, device_id_type=MESH)
+
+    def each(act):
+        def body(d, carry):
+            act(d)
+            return carry
+        lax.fori_loop(1, count, body, 0)
+
+    each(lambda d: scatter(d).start())
+    each(lambda d: scatter(d).wait_recv())
+
+    def add(d, total):
+        return total + took[d]
+
+    out_ref[me] = lax.fori_loop(1, count, add, part_ref[me])
+    each(lambda d: gather(d).start())
+    each(lambda d: landed(d).wait_recv())
+    each(lambda d: scatter(d).wait_send())
+    each(lambda d: gather(d).wait_send())
+
+
+def sum_over_bx(total):
+    count = lax.axis_size("bx")
+    rows, cols = total.shape
+    blocks = total.reshape(count, rows // count, cols)
+    vmem = pl.BlockSpec(memory_space=pltpu.VMEM)
+    return pl.pallas_call(
+        functools.partial(sum_kernel, count),
+        in_specs=[vmem],
+        out_specs=vmem,
+        out_shape=jax.ShapeDtypeStruct(blocks.shape, jnp.float32),
+        scratch_shapes=[pltpu.VMEM(blocks.shape, jnp.float32)] + [pltpu.SemaphoreType.DMA((count,))] * 4,
+        compiler_params=pltpu.CompilerParams(collective_id=0, has_side_effects=True),
+        name="sum_over_bx",
+    )(blocks).reshape(rows, cols)
 
 
 def per_device(bold, nbr_table, subject):
@@ -144,13 +228,17 @@
             pltpu.VMEM((CHUNK * GROUP, GROUP * SLOTS), jnp.bfloat16),
             pltpu.VMEM((CHUNK, epochs, SPAN), jnp.float32),
             pltpu.VMEM((CHUNK, SUBJ, SPAN), jnp.float32),
+            pltpu.VMEM((block_len, SPAN), jnp.float32),
+            pltpu.VMEM((BATCH, epochs, SPAN), jnp.bfloat16),
+            pltpu.VMEM((BATCH, epochs, SPAN), jnp.bfloat16),
+            pltpu.VMEM((BATCH, SUBJ, SPAN), jnp.float32),
         ],
         compiler_params=pltpu.CompilerParams(dimension_semantics=("arbitrary",),
                                              vmem_limit_bytes=60 * 1024 * 1024),
         name="features",
-    )(win, own, nbr_table.T, sid, hot, inv, keep)
+    )(win, own, nbr_table, sid, hot, inv, keep)
     spread = jnp.sqrt(jnp.sum(squares, axis=1) / (epochs * NB * NB))
-    gram_mean = lax.psum(total, "bx") / (NB * block_len * count)
+    gram_mean = sum_over_bx(total) / (NB * block_len * count)
     return spread, gram_mean
 
 

time: 245 us -> 123 us (0.50)
  waiting for transfers between devices: 94.8 us -> 0.01 us
  between operations: 14.2 us -> 0.77 us
  Pallas kernels: 104 us -> 92.5 us
    psum x1 -> x0, waiting for transfers between devices: 94.8 us -> none  [per_device(): gram_mean = lax.psum(total, 'bx') / (NB * block_len * count)]
    pallas_call x1, Pallas kernels: 104 us -> 67.7 us  [per_device(): pl.pallas_call(features_kernel, grid=(block_len // CHUNK,), in_specs=[vme...]
    pallas_call x0 -> x1, Pallas kernels: none -> 24.7 us  [sum_over_bx(): pl.pallas_call(functools.partial(sum_kernel, count), in_specs=[vmem], out...]
  transfers between devices with their start and end apart: 3 -> 2, of which waited for: 1 -> 0; matrix products, arithmetic and copies ran while one was open for 4% -> 6% of each run, Pallas kernels for 0% -> 0%
where the time goes in v2:
time: 123 us
  Pallas kernels  92.5 us (75%)
  local copies, waits for them, and re-layouts  13 us (11%)
  other arithmetic  12.3 us (10%)
  starting transfers between devices  4.52 us (4%)
    pallas_call x1, Pallas kernels, per_device(): pl.pallas_call(features_kernel, grid=(block_len // CHUNK,), in_specs=[vme...  67.7 us
    pallas_call x1, Pallas kernels, sum_over_bx(): pl.pallas_call(functools.partial(sum_kernel, count), in_specs=[vmem], out...  24.7 us
    ppermute x1, starting transfers between devices, per_device(): lax.ppermute(normed[:, :, block_len - LEAD:], 'bx', [(i, i + 1) for i in...  3.24 us
  transfers between devices with their start and end apart: 2, of which 0 were waited for; matrix products, arithmetic and copies ran while one was open for 6% of the time, Pallas kernels for 0%

profile of v2, /device:TPU:0, one launch (start us, length us, event | category | flops | bytes accessed | tf_op | source)
XLA Modules:
  0.0 123.1 jit_solution(6302249746026344774)
XLA Ops:
  0.6 2.0 %convert_reduce_fusion = f32[128,256]{1,0:T(8,128)S(1)} fusion(bf16[128,12,256]{2,0,1:T(8,128)(2,1)} %param.3), kind=kLoop, calls=%fused_computation.2 | loop fusion | flops 753664 | bytes 917504 | tf_op jit(solution)/shard_map/reduce_sum | solution.py:27
  2.6 2.0 %fusion.2 = f32[128,256]{1,0:T(8,128)S(1)} fusion(bf16[128,12,256]{2,0,1:T(8,128)(2,1)} %param.3, f32[128,256]{1,0:T(8,128)S(1)} %broadcast_multiply_fusion), kind=kLoop, calls=%fused_computation.6 | loop fusion | flops 1540096 | bytes 1048576 | tf_op jit(solution)/shard_map/reduce_sum | solution.py:28
  4.7 0.8 fusion.3
  5.5 0.6 pad_slice_fusion.1
  6.1 1.6 %copy.10 = bf16[128,16,160]{0,2,1:T(8,128)(2,1)} copy(bf16[128,16,160]{2,1,0:T(8,128)(2,1)S(1)} %get-tuple-element.8) | data formatting | bytes 1310720 | tf_op jit(solution)/shard_map/slice | solution.py:207
  7.7 3.2 %collective-permute-start = (bf16[128,16,160]{0,2,1:T(8,128)(2,1)}, bf16[128,16,160]{0,2,1:T(8,128)(2,1)}, u32[]{:S(2)}, u32[]{:S(2)}) collective-permute-start(bf16[128,16,160]{0,2,1:T(8,128)(2,1)} %copy.10), channel_id=1, source_target_pairs={{0,1},{1,2},{2,3},{3,4},{4,5},{5,6},{6,7},{7,8},{8,9},{9,10},{10,1... | collective-permute-start | bytes 1966088 | tf_op jit(solution)/shard_map/ppermute | solution.py:207
  10.9 1.6 %copy.11 = bf16[128,16,160]{0,2,1:T(8,128)(2,1)} copy(bf16[128,16,160]{2,1,0:T(8,128)(2,1)S(1)} %get-tuple-element.9) | data formatting | bytes 1310720 | tf_op jit(solution)/shard_map/slice | solution.py:208
  12.5 1.3 %collective-permute-start.1 = (bf16[128,16,160]{0,2,1:T(8,128)(2,1)}, bf16[128,16,160]{0,2,1:T(8,128)(2,1)}, u32[]{:S(2)}, u32[]{:S(2)}) collective-permute-start(bf16[128,16,160]{0,2,1:T(8,128)(2,1)} %copy.11), channel_id=1, source_target_pairs={{1,0},{2,1},{3,2},{4,3},{5,4},{6,5},{7,6},{8,7},{9,8},{10,9},{11,1... | collective-permute-start | bytes 1966088 | tf_op jit(solution)/shard_map/ppermute | solution.py:208
  13.9 0.2 bitcast_convert_fusion
  14.1 1.9 %copy.14 = f32[2048,256]{0,1:T(8,128)} copy(f32[2048,256]{1,0:T(8,128)S(1)} %bitcast_convert_fusion) | data formatting | bytes 4194304 | tf_op jit(solution)/shard_map/convert_element_type | solution.py:212
  16.2 0.9 reshape.36.keep_ref
  17.2 0.6 pad_convert_fusion.hot_ref
  17.8 1.8 %copy.12 = bf16[128,16,160]{2,1,0:T(8,128)(2,1)S(1)} copy(bf16[128,16,160]{0,2,1:T(8,128)(2,1)} %collective-permute-done) | data formatting | bytes 1310720 | tf_op jit(solution)/shard_map/ppermute | solution.py:207
  19.6 1.8 %copy.13 = bf16[128,16,160]{2,1,0:T(8,128)(2,1)S(1)} copy(bf16[128,16,160]{0,2,1:T(8,128)(2,1)} %collective-permute-done.1) | data formatting | bytes 1310720 | tf_op jit(solution)/shard_map/ppermute | solution.py:208
  21.4 1.3 %pad_maximum_fusion.1 = bf16[128,16,576]{2,1,0:T(8,128)(2,1)S(1)} fusion(bf16[128,16,160]{2,1,0:T(8,128)(2,1)S(1)} %copy.13, bf16[128,16,256]{2,1,0:T(8,128)(2,1)S(1)} %pad.10, bf16[128,16,160]{2,1,0:T(8,128)(2,1)S(1)} %copy.12), kind=kLoop, calls=%fused_computation.3 | loop fusion | flops 7077888 | bytes 4718592 | tf_op jit(solution)/shard_map/concatenate | solution.py:209
  22.7 1.2 slice_bitcast_fusion.1
  23.9 2.3 %pad_maximum_fusion.win_ref = bf16[2,2048,512]{2,1,0:T(8,128)(2,1)} fusion(bf16[1,2048,512]{2,1,0:T(8,128)(2,1)S(1)} %get-tuple-element.7, bf16[1,2048,512]{2,1,0:T(8,128)(2,1)S(1)} %get-tuple-element.6), kind=kLoop, calls=%fused_computation | loop fusion | flops 2097152 | bytes 8388608 | tf_op jit(solution)/shard_map/stack | solution.py:211
  26.2 0.7 broadcast_in_dim.6.sid_ref
  26.9 0.7 broadcast_in_dim.7.inv_ref
  27.6 67.7 %features.1 = (f32[256,128]{1,0:T(8,128)}, f32[128,128]{1,0:T(8,128)}) custom-call(bf16[2,2048,512]{2,1,0:T(8,128)(2,1)} %pad_maximum_fusion.win_ref, f32[256,2048]{1,0:T(8,128)} %bitcast.13, s32[128,256]{1,0:T(8,128)} %idx_ref.1, s32[128,128]{1,0:T(8,128)} %broadcast_in_dim.6.sid_ref, bf16[16,128]{1,0:T(8,128)(2,1)} %pad_convert_fusion.hot_ref, ...), custom_call_target="tpu_custom_call" | custom-call | tf_op jit(solution)/shard_map/features/pallas_call | solution.py:220
  95.3 24.7 %sum_over_bx.1 = f32[16,8,128]{2,1,0:T(8,128)} custom-call(f32[16,8,128]{2,1,0:T(8,128)} %bitcast.14), custom_call_target="tpu_custom_call" | custom-call | tf_op jit(solution)/shard_map/sum_over_bx/pallas_call | solution.py:192
  120.0 1.5 %multiply_bitcast_fusion = f32[128,128]{1,0:T(8,128)} fusion(f32[16,8,128]{2,1,0:T(8,128)} %sum_over_bx.1), kind=kLoop, calls=%fused_computation.12 | loop fusion | flops 16384 | bytes 131072 | tf_op jit(solution)/shard_map/div | solution.py:241
  121.5 1.0 reduce_sum.39
  122.5 0.6 multiply_sqrt_fusion
  (13 shorter events, 0.5 us)
Async XLA Ops:
  0.6 4.1 %copy-start = (bf16[128,12,256]{2,0,1:T(8,128)(2,1)S(1)}, bf16[128,12,256]{2,0,1:T(8,128)(2,1)}, u32[]{:S(2)}) copy-start(bf16[128,12,256]{2,0,1:T(8,128)(2,1)} %param.3) | copy-start | bytes 2359300
  7.7 10.2 %collective-permute-start = (bf16[128,16,160]{0,2,1:T(8,128)(2,1)}, bf16[128,16,160]{0,2,1:T(8,128)(2,1)}, u32[]{:S(2)}, u32[]{:S(2)}) collective-permute-start(bf16[128,16,160]{0,2,1:T(8,128)(2,1)} %copy.10), channel_id=1, source_target_pairs={{0,1},{1,2},{2,3},{3,4},{4,5},{5,6},{6,7},{7,8},{8,9},{9,10},{10,1... | collective-permute-start | bytes 1966088 | tf_op jit(solution)/shard_map/ppermute | solution.py:207
  12.5 7.1 %collective-permute-start.1 = (bf16[128,16,160]{0,2,1:T(8,128)(2,1)}, bf16[128,16,160]{0,2,1:T(8,128)(2,1)}, u32[]{:S(2)}, u32[]{:S(2)}) collective-permute-start(bf16[128,16,160]{0,2,1:T(8,128)(2,1)} %copy.11), channel_id=1, source_target_pairs={{1,0},{2,1},{3,2},{4,3},{5,4},{6,5},{7,6},{8,7},{9,8},{10,9},{11,1... | collective-permute-start | bytes 1966088 | tf_op jit(solution)/shard_map/ppermute | solution.py:208
  14.1 1.9 %copy-start.1 = (s32[128]{0:T(128)S(1)}, s32[128]{0:T(128)}, u32[]{:S(2)}) copy-start(s32[128]{0:T(128)} %param.5) | copy-start | bytes 1540

commit v3 on v2

--- a/solution.py
+++ b/solution.py
@@ -20,17 +20,53 @@
 SPAN = 384
 BATCH = 4
 MESH = pl.DeviceIdType.MESH
-
-
-def normalize(series):
-    values = series.astype(jnp.float32)
-    centred = values - jnp.mean(values, axis=1, keepdims=True)
-    divisor = jnp.sqrt(jnp.sum(centred * centred, axis=1, keepdims=True) + 1.0)
-    return (centred / divisor).astype(jnp.bfloat16)
-
-
-def features_kernel(win_ref, own_ref, idx_ref, sid_ref, hot_ref, inv_ref, keep_ref,
-                    square_ref, gram_ref, lhs_ref, prod_ref, mean_ref, root_ref, sq_ref, feat_ref, var_ref):
+BY_ROW = lax.GatherDimensionNumbers(
+    offset_dims=(), collapsed_slice_dims=(0,), start_index_map=(0,),
+    operand_batching_dims=(1,), start_indices_batching_dims=(1,))
+
+
+def normalized(raw):
+    values = raw.astype(jnp.float32)
+    points = values.shape[0]
+    centred = values - jnp.sum(values, axis=0, keepdims=True) * (1.0 / points)
+    return centred * (1.0 / jnp.sqrt(jnp.sum(centred * centred, axis=0, keepdims=True) + 1.0))
+
+
+def prepare_kernel(idx_ref, bold_ref, root_ref, own_ref, hit_ref):
+    slots, block_len = idx_ref.shape
+    points, epochs, _ = bold_ref.shape
+    depth = GROUP * SLOTS
+    for half in range(block_len // LANES):
+        place = lax.broadcasted_iota(jnp.int32, (1, LANES), 1) + half * LANES
+        shift = block_len - LEAD + place // CHUNK * CHUNK
+
+        def one_tile(w, carry):
+            at = lax.broadcasted_iota(jnp.int32, (32, LANES), 0) + w * 32 + shift
+            hits = jnp.zeros((32, LANES), jnp.float32)
+            for j in range(NB):
+                named = idx_ref[j:j + 1, half * LANES:(half + 1) * LANES]
+                hits = jnp.where(jnp.broadcast_to(named, (32, LANES)) == at, hits + 1.0, hits)
+            hit_ref[pl.ds(pl.multiple_of(w * 32, 32), 32), :] = jnp.sqrt(hits)
+            return carry
+
+        lax.fori_loop(0, SPAN // 32, one_tile, 0)
+        for t in range(SPAN // LANES):
+            root_ref[half * LANES:(half + 1) * LANES, t * LANES:(t + 1) * LANES] = (
+                hit_ref[t * LANES:(t + 1) * LANES, :].T)
+
+    def one_group(g, carry):
+        rows = pl.ds(pl.multiple_of(g * GROUP, GROUP), GROUP)
+        rounded = normalized(bold_ref[:, rows, :]).astype(jnp.bfloat16).astype(jnp.float32)
+        flat = rounded.reshape(points * GROUP, block_len)
+        flat = jnp.concatenate([flat, jnp.zeros((depth - points * GROUP, block_len), jnp.float32)], axis=0)
+        own_ref[:, pl.ds(pl.multiple_of(g * depth, depth), depth)] = flat.T
+        return carry
+
+    lax.fori_loop(0, epochs // GROUP, one_group, 0)
+
+
+def features_kernel(ext_ref, own_ref, root_ref, sid_ref, hot_ref, inv_ref, keep_ref,
+                    square_ref, gram_ref, win_ref, lhs_ref, prod_ref, mean_ref, sq_ref, feat_ref, var_ref):
     chunk = pl.program_id(0)
     first = chunk * CHUNK
     parity = lax.rem(chunk, 2)
@@ -40,31 +76,27 @@
     groups = epochs // GROUP
 
     row_epoch = lax.broadcasted_iota(jnp.int32, (GROUP, depth), 0)
-    col_epoch = lax.broadcasted_iota(jnp.int32, (GROUP, depth), 1) // SLOTS
+    col_epoch = lax.broadcasted_iota(jnp.int32, (GROUP, depth), 1) % GROUP
     diagonal = row_epoch == col_epoch
 
     @pl.when(chunk == 0)
     def _():
         gram_ref[...] = jnp.zeros_like(gram_ref)
-        slots, block_len = idx_ref.shape
-        for half in range(block_len // LANES):
-            place = lax.broadcasted_iota(jnp.int32, (1, LANES), 1) + half * LANES
-            shift = block_len - LEAD + place // CHUNK * CHUNK
-
-            def one_tile(w, carry):
-                at = lax.broadcasted_iota(jnp.int32, (32, LANES), 0) + w * 32
-                hits = jnp.zeros((32, LANES), jnp.float32)
-                for j in range(NB):
-                    rel = idx_ref[j:j + 1, half * LANES:(half + 1) * LANES] - shift
-                    hits = hits + jnp.where(jnp.broadcast_to(rel, (32, LANES)) == at, 1.0, 0.0)
-                lhs = jnp.sqrt(hits)
-                mean_ref[pl.ds(w * 4, 4), :, :LANES] = lhs.reshape(4, 8, LANES)
-                return carry
-
-            lax.fori_loop(0, SPAN // 32, one_tile, 0)
-            for t in range(SPAN // LANES):
-                tile = mean_ref[t * 16:(t + 1) * 16, :, :LANES].reshape(LANES, LANES)
-                root_ref[half * LANES:(half + 1) * LANES, t * LANES:(t + 1) * LANES] = tile.T
+        points = ext_ref.shape[0]
+        wide = win_ref.shape[2]
+        filler = jnp.zeros((depth - points * GROUP, wide), jnp.bfloat16)
+
+        def fill(g, carry):
+            rows = pl.ds(pl.multiple_of(g * GROUP, GROUP), GROUP)
+            cells = normalized(ext_ref[:, rows, :]).reshape(points * GROUP, -1)
+            base = pl.multiple_of(g * depth, depth)
+            for side in range(2):
+                win_ref[side, pl.ds(base, points * GROUP), :] = (
+                    cells[:, side * CHUNK:side * CHUNK + wide].astype(jnp.bfloat16))
+                win_ref[side, pl.ds(base + points * GROUP, depth - points * GROUP), :] = filler
+            return carry
+
+        lax.fori_loop(0, groups, fill, 0)
 
     def one_group(g, carry):
         cols = pl.ds(pl.multiple_of(g * depth, depth), depth)
@@ -101,7 +133,8 @@
     def expand(stat, r):
         at = sid_ref[r * 8:(r + 1) * 8, :]
         return jnp.concatenate(
-            [jnp.take_along_axis(stat[:, t * LANES:(t + 1) * LANES], at, axis=0, mode="promise_in_bounds")
+            [lax.gather(stat[:, t * LANES:(t + 1) * LANES], at[..., None], BY_ROW, (1, 1),
+                        mode="promise_in_bounds")
              for t in range(SPAN // LANES)], axis=1)
 
     def one_batch(p, carry):
@@ -137,7 +170,7 @@
     lax.fori_loop(0, steps + 2, one_batch, 0)
 
 
-def sum_kernel(count, part_ref, out_ref, took, send1, recv1, send2, recv2):
+def sum_kernel(count, scale, part_ref, out_ref, took, send1, recv1, send2, recv2):
     me = lax.axis_index("bx")
     barrier = pltpu.get_barrier_semaphore()
 
@@ -177,20 +210,20 @@
     def add(d, total):
         return total + took[d]
 
-    out_ref[me] = lax.fori_loop(1, count, add, part_ref[me])
+    out_ref[me] = lax.fori_loop(1, count, add, part_ref[me]) * scale
     each(lambda d: gather(d).start())
     each(lambda d: landed(d).wait_recv())
     each(lambda d: scatter(d).wait_send())
     each(lambda d: gather(d).wait_send())
 
 
-def sum_over_bx(total):
+def sum_over_bx(total, scale):
     count = lax.axis_size("bx")
     rows, cols = total.shape
     blocks = total.reshape(count, rows // count, cols)
     vmem = pl.BlockSpec(memory_space=pltpu.VMEM)
     return pl.pallas_call(
-        functools.partial(sum_kernel, count),
+        functools.partial(sum_kernel, count, scale),
         in_specs=[vmem],
         out_specs=vmem,
         out_shape=jax.ShapeDtypeStruct(blocks.shape, jnp.float32),
@@ -203,20 +236,31 @@
 def per_device(bold, nbr_table, subject):
     epochs, points, block_len = bold.shape
     count = lax.axis_size("bx")
-    normed = jnp.pad(normalize(bold), ((0, 0), (0, SLOTS - points), (0, 0)))
-    left = lax.ppermute(normed[:, :, block_len - LEAD:], "bx", [(i, i + 1) for i in range(count - 1)])
-    right = lax.ppermute(normed[:, :, :LEAD], "bx", [(i + 1, i) for i in range(count - 1)])
-    ext = jnp.concatenate([left, normed, right], axis=2).reshape(epochs * SLOTS, -1)
+    bold = bold.transpose(1, 0, 2)
+    left = lax.ppermute(bold[:, :, block_len - LEAD:], "bx", [(i, i + 1) for i in range(count - 1)])
+    right = lax.ppermute(bold[:, :, :LEAD], "bx", [(i + 1, i) for i in range(count - 1)])
+    vmem = pl.BlockSpec(memory_space=pltpu.VMEM)
     wide = SPAN + LANES
-    win = jnp.stack([ext[:, :wide], ext[:, CHUNK:CHUNK + wide]])
-    own = normed.reshape(epochs * SLOTS, block_len).T.astype(jnp.float32)
+    depth = GROUP * SLOTS
+    span = epochs * SLOTS
+    root, own = pl.pallas_call(
+        prepare_kernel,
+        in_specs=[vmem] * 2,
+        out_specs=[vmem] * 2,
+        out_shape=[jax.ShapeDtypeStruct((block_len, SPAN), jnp.float32),
+                   jax.ShapeDtypeStruct((block_len, span), jnp.float32)],
+        scratch_shapes=[pltpu.VMEM((SPAN, LANES), jnp.float32)],
+        cost_estimate=pl.CostEstimate(flops=2 * 10 ** 9, bytes_accessed=4 * 10 ** 6, transcendentals=0),
+        name="prepare",
+    )(nbr_table, bold)
+    ext = jnp.concatenate([left, bold, right], axis=2)
     onehot = subject[None, :] == jnp.arange(SUBJ, dtype=jnp.int32)[:, None]
     counts = jnp.maximum(jnp.sum(onehot.astype(jnp.float32), axis=1), 1.0)
     inv = jnp.broadcast_to((1.0 / counts)[:, None], (SUBJ, LANES))
     sid = jnp.broadcast_to(subject[:, None], (epochs, LANES))
     hot = jnp.pad(onehot.astype(jnp.bfloat16), ((0, 8), (0, 0)))
-    keep = jnp.repeat(onehot.astype(jnp.float32), SLOTS, axis=1)
-    vmem = pl.BlockSpec(memory_space=pltpu.VMEM)
+    keep = jnp.broadcast_to(onehot.astype(jnp.float32).reshape(SUBJ, -1, 1, GROUP),
+                            (SUBJ, epochs // GROUP, SLOTS, GROUP)).reshape(SUBJ, span)
     squares, total = pl.pallas_call(
         features_kernel,
         grid=(block_len // CHUNK,),
@@ -225,10 +269,10 @@
         out_shape=[jax.ShapeDtypeStruct((block_len, epochs), jnp.float32),
                    jax.ShapeDtypeStruct((epochs, epochs), jnp.float32)],
         scratch_shapes=[
-            pltpu.VMEM((CHUNK * GROUP, GROUP * SLOTS), jnp.bfloat16),
+            pltpu.VMEM((2, span, wide), jnp.bfloat16),
+            pltpu.VMEM((CHUNK * GROUP, depth), jnp.bfloat16),
             pltpu.VMEM((CHUNK, epochs, SPAN), jnp.float32),
             pltpu.VMEM((CHUNK, SUBJ, SPAN), jnp.float32),
-            pltpu.VMEM((block_len, SPAN), jnp.float32),
             pltpu.VMEM((BATCH, epochs, SPAN), jnp.bfloat16),
             pltpu.VMEM((BATCH, epochs, SPAN), jnp.bfloat16),
             pltpu.VMEM((BATCH, SUBJ, SPAN), jnp.float32),
@@ -236,9 +280,9 @@
         compiler_params=pltpu.CompilerParams(dimension_semantics=("arbitrary",),
                                              vmem_limit_bytes=60 * 1024 * 1024),
         name="features",
-    )(win, own, nbr_table, sid, hot, inv, keep)
+    )(ext, own, root, sid, hot, inv, keep)
     spread = jnp.sqrt(jnp.sum(squares, axis=1) / (epochs * NB * NB))
-    gram_mean = sum_over_bx(total) / (NB * block_len * count)
+    gram_mean = sum_over_bx(total, 1.0 / (NB * block_len * count))
     return spread, gram_mean
 
 

time: 123 us -> 107 us (0.87)
  other arithmetic: 12.3 us -> 4.51 us
  local copies, waits for them, and re-layouts: 13 us -> 7.59 us
  Pallas kernels: 92.5 us -> 89 us
    pallas_call x1, Pallas kernels: 67.7 us -> 60.7 us  [per_device(): pl.pallas_call(features_kernel, grid=(block_len // CHUNK,), in_specs=[vme...]
    reduce_sum x2 -> x0, other arithmetic: 3.97 us -> none  [the longest x1 2.01 us: normalize(): divisor = jnp.sqrt(jnp.sum(centred * centred, axis=1, keepdims=True) + 1.0)]
    pallas_call x1 -> x2, Pallas kernels: 24.7 us -> 28.4 us  [the longest x1 17.2 us: sum_over_bx(): pl.pallas_call(functools.partial(sum_kernel, count, scale), in_specs=[vme...]
    ppermute x2, local copies, waits for them, and re-layouts: 3.58 us -> 0.56 us  [the longest x1 0.28 us: per_device(): lax.ppermute(bold[:, :, :LEAD], 'bx', [(i + 1, i) for i in range(count -...]
    another operation x1 -> x0, other arithmetic: 2.29 us -> none  [per_device(): win = jnp.stack([ext[:, :wide], ext[:, CHUNK:CHUNK + wide]])]
    unnamed x4 -> x5, local copies, waits for them, and re-layouts: 0.01 us -> 2.01 us
    convert_element_type x1 -> x0, local copies, waits for them, and re-layouts: 1.86 us -> none  [per_device(): own = normed.reshape(epochs * SLOTS, block_len).T.astype(jnp.float32)]
    div x2 -> x0, other arithmetic: 1.49 us -> none  [the longest x1 1.48 us: per_device(): gram_mean = sum_over_bx(total) / (NB * block_len * count)]
  transfers between devices with their start and end apart: 2 -> 2, of which waited for: 0 -> 0; matrix products, arithmetic and copies ran while one was open for 6% -> 2% of each run, Pallas kernels for 0% -> 11%
where the time goes in v3:
time: 107 us; the launch traced here: 106 us
  Pallas kernels  89 us (83%)
  local copies, waits for them, and re-layouts  7.59 us (7%)
  other arithmetic  4.51 us (4%)
  starting transfers between devices  4.35 us (4%)
    pallas_call x1, Pallas kernels, per_device(): pl.pallas_call(features_kernel, grid=(block_len // CHUNK,), in_specs=[vme...  60.7 us
    pallas_call x1, Pallas kernels, sum_over_bx(): pl.pallas_call(functools.partial(sum_kernel, count, scale), in_specs=[vme...  17.2 us
    pallas_call x1, Pallas kernels, per_device(): pl.pallas_call(prepare_kernel, in_specs=[vmem] * 2, out_specs=[vmem] * 2,...  11.2 us
    ppermute x1, starting transfers between devices, per_device(): lax.ppermute(bold[:, :, block_len - LEAD:], 'bx', [(i, i + 1) for i in ra...  3.06 us
    slice x2, local copies, waits for them, and re-layouts, per_device(): bold[:, :, block_len - LEAD:]  2.3 us
    concatenate x1, other arithmetic, per_device(): ext = jnp.concatenate([left, bold, right], axis=2)  2.2 us
  transfers between devices with their start and end apart: 2, of which 0 were waited for; matrix products, arithmetic and copies ran while one was open for 2% of the time, Pallas kernels for 11%

profile of v3, /device:TPU:0, one launch (start us, length us, event | category | flops | bytes accessed | tf_op | source)
XLA Modules:
  0.0 106.2 jit_solution(6007765167040136051)
XLA Ops:
  0.6 0.0 copy-start.1
  0.6 1.9 %fusion.1 = (bf16[12,128,160]{2,1,0:T(8,128)(2,1)S(1)}, bf16[12,128,160]{2,1,0:T(8,128)(2,1)S(1)}) fusion(bf16[12,128,256]{2,1,0:T(8,128)(2,1)} %bitcast.5), kind=kLoop, calls=%fused_computation.8 | loop fusion | bytes 1966080 | tf_op jit(solution)/shard_map/slice | solution.py:240
  2.6 0.3 copy.6
  2.9 1.3 %collective-permute-start.1 = (bf16[12,128,160]{1,2,0:T(8,128)(2,1)S(1)}, bf16[12,128,160]{1,2,0:T(8,128)(2,1)S(1)}, u32[]{:S(2)}, u32[]{:S(2)}) collective-permute-start(bf16[12,128,160]{1,2,0:T(8,128)(2,1)S(1)} %copy.6), channel_id=1, source_target_pairs={{1,0},{2,1},{3,2},{4,3},{5,4},{6,5},{7,6},{8,7},{9,8},{10,9},{11,1... | collective-permute-start | bytes 1474568 | tf_op jit(solution)/shard_map/ppermute | solution.py:241
  4.2 0.3 copy.5
  4.6 3.1 %collective-permute-start = (bf16[12,128,160]{1,2,0:T(8,128)(2,1)S(1)}, bf16[12,128,160]{1,2,0:T(8,128)(2,1)S(1)}, u32[]{:S(2)}, u32[]{:S(2)}) collective-permute-start(bf16[12,128,160]{1,2,0:T(8,128)(2,1)S(1)} %copy.5), channel_id=1, source_target_pairs={{0,1},{1,2},{2,3},{3,4},{4,5},{5,6},{6,7},{7,8},{8,9},{9,10},{10,1... | collective-permute-start | bytes 1474568 | tf_op jit(solution)/shard_map/ppermute | solution.py:240
  7.7 0.1 eq.28
  7.8 0.6 pad_convert_fusion.hot_ref
  8.4 0.9 reshape.33.keep_ref
  9.3 0.1 convert_reduce_fusion
  9.4 11.2 %prepare.1 = (f32[256,384]{1,0:T(8,128)}, f32[256,2048]{1,0:T(8,128)}) custom-call(s32[128,256]{1,0:T(8,128)} %idx_ref.1, bf16[12,128,256]{2,1,0:T(8,128)(2,1)} %bitcast.6), custom_call_target="tpu_custom_call" | custom-call | flops 2000000000 | bytes 4000000 | tf_op jit(solution)/shard_map/prepare/pallas_call | solution.py:246
  20.6 0.0 collective-permute-done.1
  20.6 0.3 copy.8
  20.9 0.0 collective-permute-done
  20.9 0.3 copy.7
  21.2 0.5 copy-done
  21.7 2.2 %pad_maximum_fusion.ext_ref = bf16[12,128,576]{2,1,0:T(8,128)(2,1)} fusion(bf16[12,128,160]{2,1,0:T(8,128)(2,1)S(1)} %copy.8, bf16[12,128,256]{2,1,0:T(8,128)(2,1)S(1)} %bitcast.7, bf16[12,128,160]{2,1,0:T(8,128)(2,1)S(1)} %copy.7), kind=kLoop, calls=%fused_computation | loop fusion | flops 5308416 | bytes 3538944 | tf_op jit(solution)/shard_map/concatenate | solution.py:256
  23.9 0.7 broadcast_in_dim.7.inv_ref
  24.6 0.7 broadcast_in_dim.6.sid_ref
  25.3 60.7 %features.1 = (f32[256,128]{1,0:T(8,128)}, f32[128,128]{1,0:T(8,128)}) custom-call(bf16[12,128,576]{2,1,0:T(8,128)(2,1)} %pad_maximum_fusion.ext_ref, f32[256,2048]{1,0:T(8,128)} %get-tuple-element.6.own_ref, f32[256,384]{1,0:T(8,128)} %get-tuple-element.7.root_ref, s32[128,128]{1,0:T(8,128)} %broadcast_in_dim.6.sid_ref, ...), custom_call_target="tpu_custom_call" | custom-call | tf_op jit(solution)/shard_map/features/pallas_call | solution.py:264
  85.9 1.0 reduce_sum.19
  86.9 0.6 multiply_sqrt_fusion
  87.5 17.2 %sum_over_bx.1 = f32[16,8,128]{2,1,0:T(8,128)} custom-call(f32[16,8,128]{2,1,0:T(8,128)} %bitcast.9), custom_call_target="tpu_custom_call" | custom-call | tf_op jit(solution)/shard_map/sum_over_bx/pallas_call | solution.py:225
  104.7 1.5 %copy.10 = f32[128,128]{1,0:T(8,128)} copy(f32[128,128]{1,0:T(8,128)} %bitcast.8) | data formatting | bytes 131072
  (6 shorter events, 0.1 us)
Async XLA Ops:
  0.6 7.0 %copy-start.1 = (s32[128]{0:T(128)S(1)}, s32[128]{0:T(128)}, u32[]{:S(2)}) copy-start(s32[128]{0:T(128)} %param.5) | copy-start | bytes 1540
  2.9 17.6 %collective-permute-start.1 = (bf16[12,128,160]{1,2,0:T(8,128)(2,1)S(1)}, bf16[12,128,160]{1,2,0:T(8,128)(2,1)S(1)}, u32[]{:S(2)}, u32[]{:S(2)}) collective-permute-start(bf16[12,128,160]{1,2,0:T(8,128)(2,1)S(1)} %copy.6), channel_id=1, source_target_pairs={{1,0},{2,1},{3,2},{4,3},{5,4},{6,5},{7,6},{8,7},{9,8},{10,9},{11,1... | collective-permute-start | bytes 1474568 | tf_op jit(solution)/shard_map/ppermute | solution.py:241
  4.6 16.3 %collective-permute-start = (bf16[12,128,160]{1,2,0:T(8,128)(2,1)S(1)}, bf16[12,128,160]{1,2,0:T(8,128)(2,1)S(1)}, u32[]{:S(2)}, u32[]{:S(2)}) collective-permute-start(bf16[12,128,160]{1,2,0:T(8,128)(2,1)S(1)} %copy.5), channel_id=1, source_target_pairs={{0,1},{1,2},{2,3},{3,4},{4,5},{5,6},{6,7},{7,8},{8,9},{9,10},{10,1... | collective-permute-start | bytes 1474568 | tf_op jit(solution)/shard_map/ppermute | solution.py:240
  20.6 1.1 %copy-start = (bf16[128,12,256]{2,0,1:T(8,128)(2,1)S(1)}, bf16[128,12,256]{2,0,1:T(8,128)(2,1)}, u32[]{:S(2)}) copy-start(bf16[128,12,256]{2,0,1:T(8,128)(2,1)} %param.3) | copy-start | bytes 2359300
